TPU v7x, 32 devices: a whole 2x2x4 slice. The times are simulated.
32 devices in a mesh: rep: 4 (over y, core), ep: 4 (over z), tp: 2 (over x).
Axes of the slice: x: 2, y: 2, z: 4, core: 2. Of those that a mesh axis runs over, the one named last changes fastest.
Arguments:
- tokens: bfloat16 [128, 6144], P(('rep', 'ep'), 'tp'), may hold values from -6 to 6
- expert_ids: int32 [128, 2], P(('rep', 'ep')), may hold values from 0 to 3, as said below
- replicas: int32 [128, 2], P(('rep', 'ep')), may hold values from 0 to 3, as said below
- scores: float32 [128, 2], P(('rep', 'ep')), may hold values from -8 to 8
- w_gate: bfloat16 [4, 6144, 1024], P('ep', None, 'tp'), may hold values from -0.078125 to 0.078125
- w_up: bfloat16 [4, 6144, 1024], P('ep', None, 'tp'), may hold values from -0.078125 to 0.078125
- w_down: bfloat16 [4, 1024, 6144], P('ep', 'tp'), may hold values from -0.1875 to 0.1875
Outputs:
- moe_out: bfloat16 [128, 6144], P(('rep', 'ep'), 'tp')
- load_counts: int32 [4, 4], replicated
Inputs may be any that keep to these rules, and one draw needn't show every extreme that they name: `expert_ids`: each row names 2 different experts. In the rows of one device one expert is named by every row. `replicas`: in the rows of one device at most 2 pairs name the same expert with the same replica pick, and some expert and pick reach 2.
All inputs are finite; a program needn't handle non-finite values.
Results may differ from a plain program's by a relative error of at most 0.008.
Values may be sent and summed in bfloat16 or wider, within the bound.
A program may use at most 64 MiB of HBM per device.

v0:
```python
import functools

import jax
import jax.numpy as jnp
from jax import lax
from jax.experimental import pallas as pl
from jax.experimental.pallas import tpu as pltpu
from jax.sharding import PartitionSpec as P

REPL = 4
route_scale = 2.5
GATHER_CHUNKS = 3
RETURN_CHUNKS = 4
MESH = pl.DeviceIdType.MESH


def stable_sigmoid(v):
    small = jnp.exp(-jnp.abs(v))
    return jnp.where(v >= 0, 1.0, small) / (1.0 + small)


def kernel(
    sizes,
    tokens_hbm, ids_hbm, replicas_hbm, scores_hbm, gate_hbm, up_hbm, down_hbm,
    out_ref, counts_ref,
    ids_ref, replicas_ref, scores_ref,
    x_buf, gate_buf, up_buf, down_buf,
    own_sum, tp_send, tp_recv, ep_send, ep_recv,
    count_own, count_ep, count_mid, count_rep,
    token_sem, table_sem, weight_sem,
    gather_recv, gather_ep_send, gather_tp_send,
    tp_send_sem, tp_recv_sem, ep_send_sem, ep_recv_sem,
    count_ep_send, count_ep_recv, count_rep_send, count_rep_recv,
):
    reps, eps, tps, rows, width = sizes
    stride = reps // REPL
    me_rep, me_ep, me_tp = lax.axis_index("rep"), lax.axis_index("ep"), lax.axis_index("tp")
    rep_peer = lambda o: {"rep": lax.rem(me_rep + o, reps)}
    ep_peer = lambda o: {"ep": lax.rem(me_ep + o, eps)}
    tp_peer = lambda o: {"tp": lax.rem(me_tp + o, tps)}
    g_chunk = width // GATHER_CHUNKS
    r_chunk = width // RETURN_CHUNKS
    top_k = ids_ref.shape[0]

    def remote(src, dst, send, recv, device):
        return pltpu.make_async_remote_copy(
            src_ref=src, dst_ref=dst, send_sem=send, recv_sem=recv,
            device_id=device, device_id_type=MESH,
        )

    barrier = pltpu.get_barrier_semaphore()
    peers = (
        [ep_peer(o) for o in range(1, eps)]
        + [tp_peer(o) for o in range(1, tps)]
        + [rep_peer(o) for o in range(1, reps)]
    )
    for peer in peers:
        pl.semaphore_signal(barrier, inc=1, device_id=peer, device_id_type=MESH)

    token_copies = []
    for c in range(GATHER_CHUNKS):
        copy = pltpu.make_async_copy(
            tokens_hbm.at[:, pl.ds(c * g_chunk, g_chunk)], x_buf.at[0, c, 0], token_sem.at[c]
        )
        copy.start()
        token_copies.append(copy)
    table_copies = []
    for k, (src, dst) in enumerate(((ids_hbm, ids_ref), (replicas_hbm, replicas_ref), (scores_hbm, scores_ref))):
        copy = pltpu.make_async_copy(src, dst, table_sem.at[k])
        copy.start()
        table_copies.append(copy)

    for copy in token_copies + table_copies:
        copy.wait()
    weight_copies = {}
    for d in range(tps):
        start = pl.multiple_of(lax.rem(me_tp + d, tps) * width, width)
        for k, (src, dst) in enumerate(((gate_hbm, gate_buf), (up_hbm, up_buf))):
            copy = pltpu.make_async_copy(src.at[0, pl.ds(start, width), :], dst.at[d], weight_sem.at[k, d])
            copy.start()
            weight_copies[k, d] = copy
    for d in list(range(1, tps)) + [0]:
        start = pl.multiple_of(lax.rem(me_tp + d, tps) * width, width)
        copy = pltpu.make_async_copy(down_hbm.at[0, :, pl.ds(start, width)], down_buf.at[d], weight_sem.at[2, d])
        copy.start()
        weight_copies[2, d] = copy

    diagonal = lax.broadcasted_iota(jnp.int32, (rows, rows), 0) == lax.broadcasted_iota(jnp.int32, (rows, rows), 1)

    def columns(ref):
        table = ref[...]
        zero = jnp.zeros((), table.dtype)
        return [
            jnp.sum(jnp.where(diagonal, table[k : k + 1, :], zero), 1, keepdims=True)
            for k in range(top_k)
        ]

    ids = columns(ids_ref)
    target = [lax.rem(me_rep + r * stride, reps) for r in columns(replicas_ref)]
    expert_lane = lax.broadcasted_iota(jnp.int32, (rows, count_own.shape[1]), 1)
    count_own[...] = jnp.zeros_like(count_own)
    hits = [ids[k] == expert_lane for k in range(top_k)]
    for g in range(reps):
        total = jnp.zeros(expert_lane.shape, jnp.float32)
        for k in range(top_k):
            total += jnp.where(hits[k] & (target[k] == g), 1.0, 0.0)
        count_own[g : g + 1, :] = jnp.sum(total, 0, keepdims=True).astype(jnp.int32)

    sigmoid_scores = [stable_sigmoid(v) for v in columns(scores_ref)]
    norm = sum(sigmoid_scores)
    weights = [v / norm * route_scale for v in sigmoid_scores]
    coefficients = []
    for s in range(eps):
        expert = lax.rem(me_ep + s, eps)
        coefficients.append(sum(jnp.where(ids[k] == expert, weights[k], 0.0) for k in range(top_k)))

    pl.semaphore_wait(barrier, len(peers))
    pending = []

    for c in range(GATHER_CHUNKS):
        for o in range(eps - 1, 0, -1):
            copy = remote(
                x_buf.at[0, c, 0], x_buf.at[0, c, eps - o],
                gather_ep_send.at[c, o], gather_recv.at[0, c, eps - o], ep_peer(o),
            )
            copy.start()
            pending.append(copy)
        for d in range(1, tps):
            copy = remote(
                x_buf.at[0, c, 0], x_buf.at[tps - d, c, 0],
                gather_tp_send.at[d, c, 0], gather_recv.at[tps - d, c, 0], tp_peer(d),
            )
            copy.start()
            pending.append(copy)

    def gather_wait(d, c, s):
        pltpu.make_async_copy(x_buf.at[d, c, s], x_buf.at[d, c, s], gather_recv.at[d, c, s]).wait()

    count_copies = []
    for o in range(1, eps):
        copy = remote(count_own, count_ep.at[o], count_ep_send.at[o], count_ep_recv.at[o], ep_peer(o))
        copy.start()
        count_copies.append(copy)

    for c in range(GATHER_CHUNKS):
        for o in range(eps - 1, 0, -1):
            s = eps - o
            gather_wait(0, c, s)
            for d in range(1, tps):
                copy = remote(
                    x_buf.at[0, c, s], x_buf.at[tps - d, c, s],
                    gather_tp_send.at[d, c, s], gather_recv.at[tps - d, c, s], tp_peer(d),
                )
                copy.start()
                pending.append(copy)

    hidden_count = gate_buf.shape[2]
    gate = jnp.zeros((eps * rows, hidden_count), jnp.float32)
    up = jnp.zeros((eps * rows, hidden_count), jnp.float32)
    for d in range(tps):
        for k in range(2):
            weight_copies[k, d].wait()
        for c in range(GATHER_CHUNKS):
            if d > 0:
                for s in range(eps):
                    gather_wait(d, c, s)
            x = x_buf[d, c].astype(jnp.float32).reshape(eps * rows, g_chunk).astype(jnp.bfloat16)
            gate += jnp.dot(x, gate_buf[d, pl.ds(c * g_chunk, g_chunk), :], preferred_element_type=jnp.float32)
            up += jnp.dot(x, up_buf[d, pl.ds(c * g_chunk, g_chunk), :], preferred_element_type=jnp.float32)
    hidden = (gate * stable_sigmoid(gate) * up).astype(jnp.bfloat16)

    mid = count_own[...]
    for o in range(1, eps):
        count_copies[o - 1].wait_recv()
        mid += count_ep[o]
    count_mid[...] = mid
    rep_copies = []
    for o in range(1, reps):
        copy = remote(count_mid, count_rep.at[o], count_rep_send.at[o], count_rep_recv.at[o], rep_peer(o))
        copy.start()
        rep_copies.append(copy)

    tp_copies = {}
    for d in list(range(1, tps)) + [0]:
        weight_copies[2, d].wait()
        for c in range(RETURN_CHUNKS):
            part = jnp.dot(hidden, down_buf[d, :, pl.ds(c * r_chunk, r_chunk)], preferred_element_type=jnp.float32)
            part = part.reshape(eps, rows, r_chunk)
            if d == 0:
                own_sum[c] = part
                continue
            tp_send[d - 1, c] = part.astype(jnp.bfloat16)
            copy = remote(
                tp_send.at[d - 1, c], tp_recv.at[d - 1, c],
                tp_send_sem.at[d - 1, c], tp_recv_sem.at[d - 1, c], tp_peer(d),
            )
            copy.start()
            tp_copies[d, c] = copy

    ep_copies = {}
    for c in range(RETURN_CHUNKS):
        total = own_sum[c]
        for d in range(1, tps):
            tp_copies[d, c].wait_recv()
            total += tp_recv[d - 1, c].astype(jnp.float32)
        ep_send[c] = total.astype(jnp.bfloat16)
        for o in range(1, eps):
            copy = remote(
                ep_send.at[c, o], ep_recv.at[c, eps - o],
                ep_send_sem.at[c, o], ep_recv_sem.at[c, eps - o], ep_peer(o),
            )
            copy.start()
            ep_copies[c, o] = copy

    final = count_mid[...]
    for o in range(1, reps):
        rep_copies[o - 1].wait_recv()
        final += count_rep[o]
    counts_ref[...] = final[:reps, :eps]

    for c in range(RETURN_CHUNKS):
        total = coefficients[0] * ep_send[c, 0].astype(jnp.float32)
        for s in range(1, eps):
            pltpu.make_async_copy(ep_recv.at[c, s], ep_recv.at[c, s], ep_recv_sem.at[c, s]).wait()
            total += coefficients[s] * ep_recv[c, s].astype(jnp.float32)
        out_ref[:, pl.ds(c * r_chunk, r_chunk)] = total.astype(out_ref.dtype)

    for copy in pending + count_copies + rep_copies + list(tp_copies.values()) + list(ep_copies.values()):
        copy.wait_send()


def per_device(tokens, expert_ids, replicas, scores, w_gate, w_up, w_down):
    reps, eps, tps = lax.axis_size("rep"), lax.axis_size("ep"), lax.axis_size("tp")
    rows, width = tokens.shape
    hidden = w_gate.shape[2]
    g_chunk, r_chunk = width // GATHER_CHUNKS, width // RETURN_CHUNKS
    sizes = (reps, eps, tps, rows, width)
    vmem = pl.BlockSpec(memory_space=pltpu.VMEM)
    hbm = pl.BlockSpec(memory_space=pl.ANY)
    lanes = 128
    count_rows = -(-reps // 8) * 8
    dma = pltpu.SemaphoreType.DMA
    bf16, f32, i32 = jnp.bfloat16, jnp.float32, jnp.int32
    moe, counts = pl.pallas_call(
        functools.partial(kernel, sizes),
        out_shape=(
            pltpu.VMEM((rows, width), bf16),
            pltpu.VMEM((reps, eps), i32),
        ),
        in_specs=[hbm] * 7,
        out_specs=(vmem, vmem),
        scratch_shapes=[
            pltpu.VMEM(expert_ids.shape[::-1], i32),
            pltpu.VMEM(replicas.shape[::-1], i32),
            pltpu.VMEM(scores.shape[::-1], f32),
            pltpu.VMEM((tps, GATHER_CHUNKS, eps, rows, g_chunk), bf16),
            pltpu.VMEM((tps, width, hidden), bf16),
            pltpu.VMEM((tps, width, hidden), bf16),
            pltpu.VMEM((tps, hidden, width), bf16),
            pltpu.VMEM((RETURN_CHUNKS, eps, rows, r_chunk), f32),
            pltpu.VMEM((tps - 1, RETURN_CHUNKS, eps, rows, r_chunk), bf16),
            pltpu.VMEM((tps - 1, RETURN_CHUNKS, eps, rows, r_chunk), bf16),
            pltpu.VMEM((RETURN_CHUNKS, eps, rows, r_chunk), bf16),
            pltpu.VMEM((RETURN_CHUNKS, eps, rows, r_chunk), bf16),
            pltpu.VMEM((count_rows, lanes), i32),
            pltpu.VMEM((eps, count_rows, lanes), i32),
            pltpu.VMEM((count_rows, lanes), i32),
            pltpu.VMEM((reps, count_rows, lanes), i32),
            dma((GATHER_CHUNKS,)),
            dma((3,)),
            dma((3, tps)),
            dma((tps, GATHER_CHUNKS, eps)),
            dma((GATHER_CHUNKS, eps)),
            dma((tps, GATHER_CHUNKS, eps)),
            dma((tps - 1, RETURN_CHUNKS)),
            dma((tps - 1, RETURN_CHUNKS)),
            dma((RETURN_CHUNKS, eps)),
            dma((RETURN_CHUNKS, eps)),
            dma((eps,)),
            dma((eps,)),
            dma((reps,)),
            dma((reps,)),
        ],
        compiler_params=pltpu.CompilerParams(
            collective_id=0, has_side_effects=True, vmem_limit_bytes=56 * 1024 * 1024
        ),
    )(tokens, expert_ids.T, replicas.T, scores.T, w_gate, w_up, w_down)
    return moe, counts


def solution(mesh):
    placed = (
        P(("rep", "ep"), "tp"),
        P(("rep", "ep"), None),
        P(("rep", "ep"), None),
        P(("rep", "ep"), None),
        P("ep", None, "tp"),
        P("ep", None, "tp"),
        P("ep", "tp", None),
    )
    return jax.shard_map(
        per_device,
        mesh=mesh,
        in_specs=placed,
        out_specs=(P(("rep", "ep"), "tp"), P()),
        check_vma=False,
    )
```

profile of v0, /device:TPU:0, one launch (start us, length us, event | category | flops | bytes accessed | tf_op | source)
XLA Modules:
  0.0 25.7 jit_solution(2182080565079653817)
XLA Ops:
  0.6 23.9 %shard_map.86 = (bf16[8,3072]{1,0:T(8,128)(2,1)S(1)}, s32[4,4]{1,0:T(4,128)S(1)}) custom-call(bf16[8,3072]{1,0:T(8,128)(2,1)} %tokens_hbm.1, s32[2,8]{1,0:T(2,128)} %bitcast.3, s32[2,8]{1,0:T(2,128)} %bitcast.4, f32[2,8]{1,0:T(2,128)} %bitcast.5, bf16[1,6144,512]{2,1,0:T(8,128)(2,1)} %gate_hbm.1, bf16[1,6144,512]{2,1,0:T(8,128)(2,1)} %up_hbm.1, ...), custom_call_target="tpu_custom_call" | custom-call | tf_op jit(solution)/shard_map/pallas_call | solution.py:244
  24.5 0.6 %copy.11 = bf16[8,3072]{1,0:T(8,128)(2,1)} copy(bf16[8,3072]{1,0:T(8,128)(2,1)S(1)} %get-tuple-element.2) | data formatting | bytes 98304
  25.2 0.6 %copy.12 = s32[4,4]{1,0:T(4,128)} copy(s32[4,4]{1,0:T(4,128)S(1)} %get-tuple-element.3) | data formatting | bytes 128
where the time goes:
time: 26 us; the launch traced here: 25.7 us
  Pallas kernels  23.9 us (92%)
  local copies, waits for them, and re-layouts  1.2 us (5%)
  between operations  0.64 us (2%)
    pallas_call x1, Pallas kernels, per_device(): pl.pallas_call(functools.partial(kernel, sizes), out_shape=(pltpu.VMEM((r...  23.9 us
    unnamed x2, local copies, waits for them, and re-layouts  1.2 us

commit v1 on v0

--- a/solution.py
+++ b/solution.py
@@ -285,7 +285,22 @@
             collective_id=0, has_side_effects=True, vmem_limit_bytes=56 * 1024 * 1024
         ),
     )(tokens, expert_ids.T, replicas.T, scores.T, w_gate, w_up, w_down)
-    return moe, counts
+    return pl.pallas_call(
+        finish,
+        out_shape=(jax.ShapeDtypeStruct(moe.shape, moe.dtype), jax.ShapeDtypeStruct(counts.shape, counts.dtype)),
+        in_specs=[vmem, vmem],
+        out_specs=(hbm, hbm),
+        scratch_shapes=[dma((2,))],
+    )(pltpu.with_memory_space_constraint(moe, pltpu.VMEM), pltpu.with_memory_space_constraint(counts, pltpu.VMEM))
+
+
+def finish(moe_ref, counts_ref, moe_out, counts_out, sem):
+    a = pltpu.make_async_copy(moe_ref, moe_out, sem.at[0])
+    b = pltpu.make_async_copy(counts_ref, counts_out, sem.at[1])
+    a.start()
+    b.start()
+    a.wait()
+    b.wait()
 
 
 def solution(mesh):

time: 26 us -> 25.4 us (0.977)
  local copies, waits for them, and re-layouts: 1.2 us -> 0 us
  Pallas kernels: 23.9 us -> 24.5 us
    unnamed x2 -> x0, local copies, waits for them, and re-layouts: 1.2 us -> none
    pallas_call x0 -> x1, Pallas kernels: none -> 0.64 us  [per_device(): pl.pallas_call(finish, out_shape=(jax.ShapeDtypeStruct(moe.shape, moe.dty...]
where the time goes in v1:
time: 25.4 us; the launch traced here: 25.2 us
  Pallas kernels  24.5 us (96%)
  between operations  0.64 us (3%)
    pallas_call x1, Pallas kernels, per_device(): pl.pallas_call(functools.partial(kernel, sizes), out_shape=(pltpu.VMEM((r...  23.9 us
    pallas_call x1, Pallas kernels, per_device(): pl.pallas_call(finish, out_shape=(jax.ShapeDtypeStruct(moe.shape, moe.dty...  0.64 us

profile of v1, /device:TPU:0, one launch (start us, length us, event | category | flops | bytes accessed | tf_op | source)
XLA Modules:
  0.0 25.2 jit_solution(8706559066388629045)
XLA Ops:
  0.6 23.9 %shard_map.86 = (bf16[8,3072]{1,0:T(8,128)(2,1)S(1)}, s32[4,4]{1,0:T(4,128)S(1)}) custom-call(bf16[8,3072]{1,0:T(8,128)(2,1)} %tokens_hbm.1, s32[2,8]{1,0:T(2,128)} %bitcast.3, s32[2,8]{1,0:T(2,128)} %bitcast.4, f32[2,8]{1,0:T(2,128)} %bitcast.5, bf16[1,6144,512]{2,1,0:T(8,128)(2,1)} %gate_hbm.1, bf16[1,6144,512]{2,1,0:T(8,128)(2,1)} %up_hbm.1, ...), custom_call_target="tpu_custom_call" | custom-call | tf_op jit(solution)/shard_map/pallas_call | solution.py:244
  24.5 0.6 %shard_map.87 = (bf16[8,3072]{1,0:T(8,128)(2,1)}, s32[4,4]{1,0:T(4,128)}) custom-call(bf16[8,3072]{1,0:T(8,128)(2,1)S(1)} %get-tuple-element.4.moe_ref, s32[4,4]{1,0:T(4,128)S(1)} %get-tuple-element.5.counts_ref), custom_call_target="tpu_custom_call" | custom-call | tf_op jit(solution)/shard_map/pallas_call | solution.py:288
